TPU v7x, 32 devices: a whole 2x2x4 slice. The times are simulated.
32 devices in a mesh: groups: 1, role: 2 (over core), dev: 16 (over z, y, x).
Axes of the slice: x: 2, y: 2, z: 4, core: 2. Of those that a mesh axis runs over, the one named last changes fastest.
Arguments:
- prompt_hidden: bfloat16 [4096, 4096], P(('groups', 'dev')), may hold values from -6 to 6
- norm_gain: float32 [4096], replicated, may hold values from 0.25 to 1.75
- kv_weight: bfloat16 [4096, 4, 2, 128], P(None, 'role'), may hold values from -0.09375 to 0.09375
- prompt_excess: int32 [4], P('groups'), may hold values from 1 to 1536, 2048 in all
- prompt_owner: int32 [4], P('groups'), may hold values from 0 to 15, as said below
- response_counts: int32 [4], P('groups'), may hold values from 1 to 5, as said below
- queries: bfloat16 [256, 16, 128], P(('groups', 'dev'), 'role'), may hold values from -256 to 256
- new_kv: bfloat16 [256, 4, 2, 128], P(('groups', 'dev'), 'role'), may hold values from -6 to 6
- response_cache: bfloat16 [256, 256, 4, 2, 128], P(('groups', 'dev'), None, 'role'), may hold values from -6 to 6
- positions: int32 [256], P(('groups', 'dev')), may hold values from 0 to 256
- out_weight: bfloat16 [16, 128, 4096], P('role', None, 'dev'), may hold values from -0.125 to 0.125
Outputs:
- attended: bfloat16 [256, 16, 128], P(('groups', 'dev'), 'role')
- block_out: bfloat16 [256, 4096], P(('groups', 'role'), 'dev')
Inputs may be any that keep to these rules, and one draw needn't show every extreme that they name: `prompt_owner`: no device along dev owns more than two prompts, and some device owns exactly two. `response_counts`: some prompt has exactly 5 responses.
All inputs are finite; a program needn't handle non-finite values.
Results may differ from a plain program's by a relative error of at most 0.0065.
Values may be sent and summed in bfloat16 or wider, within the bound.
No kernel may reach another device: no remote copies, remote signals or barrier semaphores. Data moves between devices by JAX's collectives and lax.ppermute only.
A program may use at most 192 MiB of HBM per device.

v0:
```python
import jax
import jax.numpy as jnp
from jax import lax
from jax.sharding import PartitionSpec as P

RESP = 5
PROMPT_MIN = 512
rope_base = 500000.0


def merged_2(part, axis, combine):
    gathered = jax.tree.map(lambda a: lax.all_gather(a, axis), part)

    def take(source):
        return jax.tree.map(lambda a: lax.dynamic_index_in_dim(a, source, 0, False), gathered)

    return lax.fori_loop(
        1, lax.axis_size(axis), lambda source, state: combine(state, take(source)), take(0)
    )


def rotate(vectors, offsets):
    half = vectors.shape[-1] // 2
    freq = rope_base ** (-jnp.arange(half, dtype=jnp.float32) * 2.0 / vectors.shape[-1])
    angles = offsets.astype(jnp.float32)[:, None] * freq[None, :]
    cosine = jnp.cos(angles)[:, None, :]
    sine = jnp.sin(angles)[:, None, :]
    first = vectors[..., :half]
    second = vectors[..., half:]
    return jnp.concatenate(
        [first * cosine - second * sine, second * cosine + first * sine], axis=-1
    )


def prompt_layout(prompt_excess, token_index):
    lengths = PROMPT_MIN + prompt_excess
    ends = jnp.cumsum(lengths)
    starts = ends - lengths
    prompt_id = jnp.sum((token_index[:, None] >= ends[None, :]).astype(jnp.int32), axis=1)
    member = prompt_id[:, None] == jnp.arange(lengths.shape[0], dtype=jnp.int32)[None, :]
    offsets = token_index - jnp.sum(jnp.where(member, starts[None, :], 0), axis=1)
    return (member, offsets, starts, lengths)


def first_slots(owner, counts):
    order = jnp.arange(owner.shape[0], dtype=jnp.int32)
    earlier = (owner[:, None] == owner[None, :]) & (order[None, :] < order[:, None])
    return jnp.sum(jnp.where(earlier, counts[None, :], 0), axis=1)


def slot_prompts(owner, counts, slot_device, slot_index):
    order = jnp.arange(owner.shape[0], dtype=jnp.int32)
    first = first_slots(owner, counts)
    match = (
        (owner[None, :] == slot_device[:, None])
        & (first[None, :] <= slot_index[:, None])
        & (slot_index[:, None] < first[None, :] + counts[None, :])
    )
    present = jnp.any(match, axis=1)
    chosen = jnp.sum(jnp.where(match, order[None, :], 0), axis=1)
    return (chosen, present)


def softmax_state(scores, valid):
    scores = jnp.where(valid[:, None, None, :], scores, -1e30)
    peak = jnp.max(scores, axis=-1)
    weights = jnp.where(valid[:, None, None, :], jnp.exp(scores - peak[..., None]), 0.0)
    return (peak, jnp.sum(weights, axis=-1), weights.astype(jnp.bfloat16))


def state_each(query, keys, values, valid, scale):
    scores = jnp.einsum("sngd,slnd->sngl", query, keys, preferred_element_type=jnp.float32) * scale
    peak, total, rounded = softmax_state(scores, valid)
    mixed = jnp.einsum("sngl,slnd->sngd", rounded, values, preferred_element_type=jnp.float32)
    return (peak, total, mixed)


def state_shared(query, keys, values, valid, scale):
    scores = jnp.einsum("sngd,lnd->sngl", query, keys, preferred_element_type=jnp.float32) * scale
    peak, total, rounded = softmax_state(scores, valid)
    mixed = jnp.einsum("sngl,lnd->sngd", rounded, values, preferred_element_type=jnp.float32)
    return (peak, total, mixed)


def combine(first, second):
    peak = jnp.maximum(first[0], second[0])
    left_scale = jnp.exp(first[0] - peak)
    right_scale = jnp.exp(second[0] - peak)
    total = first[1] * left_scale + second[1] * right_scale
    mixed = first[2] * left_scale[..., None] + second[2] * right_scale[..., None]
    return (peak, total, mixed)


def on_device(
    prompt_hidden,
    norm_gain,
    kv_weight,
    prompt_excess,
    prompt_owner,
    response_counts,
    queries,
    new_kv,
    response_cache,
    positions,
    out_weight,
):
    device = lax.axis_index("dev")
    rows = prompt_hidden.shape[0]
    width = prompt_hidden.shape[1]
    local_heads = kv_weight.shape[1]
    head_size = kv_weight.shape[3]
    slots = queries.shape[0]
    query_heads = queries.shape[1]
    group = query_heads // local_heads
    prompt_count = prompt_excess.shape[0]
    scale = head_size ** (-0.5)
    token_index = device * rows + jnp.arange(rows, dtype=jnp.int32)
    member, offsets, starts, lengths = prompt_layout(prompt_excess, token_index)
    hidden = prompt_hidden.astype(jnp.float32)
    normed = (
        hidden * lax.rsqrt(jnp.mean(hidden * hidden, axis=-1, keepdims=True) + 1e-05) * norm_gain
    ).astype(jnp.bfloat16)
    projected = jnp.dot(
        normed,
        kv_weight.reshape(width, local_heads * 2 * head_size),
        preferred_element_type=jnp.float32,
    )
    projected = projected.reshape(rows, local_heads, 2, head_size)
    prompt_keys = rotate(projected[:, :, 0], offsets).astype(jnp.bfloat16)
    prompt_values = projected[:, :, 1].astype(jnp.bfloat16)
    grouped = queries.reshape(slots, local_heads, group, head_size)
    slot_index = jnp.arange(slots, dtype=jnp.int32)
    chosen, present = slot_prompts(
        prompt_owner, response_counts, jnp.zeros((slots,), jnp.int32) + device, slot_index
    )
    cache_valid = jnp.arange(response_cache.shape[1], dtype=jnp.int32)[None, :] < positions[:, None]
    cache_state = state_each(
        grouped, response_cache[:, :, :, 0], response_cache[:, :, :, 1], cache_valid, scale
    )
    self_valid = jnp.ones((slots, 1), dtype=bool)
    self_state = state_each(
        grouped, new_kv[:, None, :, 0], new_kv[:, None, :, 1], self_valid, scale
    )
    first = first_slots(prompt_owner, response_counts)
    rank = jnp.clip(slot_index - first[chosen], 0, RESP - 1)
    entry = chosen * RESP + rank
    select = (
        (entry[None, :] == jnp.arange(prompt_count * RESP, dtype=jnp.int32)[:, None])
        & present[None, :]
    ).astype(jnp.float32)
    table = jnp.dot(
        select,
        queries.reshape(slots, query_heads * head_size).astype(jnp.float32),
        precision=lax.Precision.HIGHEST,
    )
    table = lax.psum(table, "dev").astype(jnp.bfloat16)
    table = table.reshape(prompt_count, RESP, local_heads, group, head_size)
    held = jnp.any(member, axis=0)
    first_prompt = jnp.sum((starts + lengths <= token_index[0]).astype(jnp.int32))
    reach = min(rows // PROMPT_MIN + 2, prompt_count)
    layout = (
        jnp.full((prompt_count, RESP, local_heads, group), -1e30, jnp.float32),
        jnp.zeros((prompt_count, RESP, local_heads, group), jnp.float32),
        jnp.zeros((prompt_count, RESP, local_heads, group, head_size), jnp.float32),
    )
    for step in range(reach):
        pick = jnp.minimum(first_prompt + step, prompt_count - 1)
        live = (first_prompt + step < prompt_count) & held[pick]
        reply_queries = lax.dynamic_index_in_dim(table, pick, 0, keepdims=False)
        reply_live = jnp.arange(RESP, dtype=jnp.int32) < response_counts[pick]
        row_member = (token_index >= starts[pick]) & (token_index < starts[pick] + lengths[pick])
        valid = live & reply_live[:, None] & row_member[None, :]
        fresh = state_shared(reply_queries, prompt_keys, prompt_values, valid, scale)
        earlier = tuple(
            (lax.dynamic_index_in_dim(part_now, pick, 0, keepdims=False) for part_now in layout)
        )
        merged = combine(earlier, fresh)
        layout = tuple(
            (
                lax.dynamic_update_index_in_dim(part_now, part_new, pick, 0)
                for part_now, part_new in zip(layout, merged)
            )
        )
    joined_peak, joined_total, joined_mixed = merged_2(layout, "dev", combine)
    flat_peak = joined_peak.reshape(prompt_count * RESP, local_heads, group)
    flat_total = joined_total.reshape(prompt_count * RESP, local_heads, group)
    flat_mixed = joined_mixed.reshape(prompt_count * RESP, local_heads, group, head_size)
    own_peak = jnp.take(flat_peak, entry, axis=0)
    own_total = jnp.take(flat_total, entry, axis=0)
    own_mixed = jnp.take(flat_mixed, entry, axis=0)
    prompt_state = (
        jnp.where(present[:, None, None], own_peak, -1e30),
        jnp.where(present[:, None, None], own_total, 0.0),
        jnp.where(present[:, None, None, None], own_mixed, 0.0),
    )
    final = combine(combine(prompt_state, cache_state), self_state)
    attended = (
        (final[2] / final[1][..., None]).reshape(slots, query_heads, head_size).astype(jnp.bfloat16)
    )
    flat = attended.reshape(slots, query_heads * head_size)
    weight_flat = out_weight.reshape(query_heads * head_size, out_weight.shape[2])
    head_terms = jnp.dot(
        lax.all_gather(flat, "dev", axis=0, tiled=True),
        weight_flat,
        preferred_element_type=jnp.float32,
    )
    block_out = lax.psum_scatter(head_terms, "role", scatter_dimension=0, tiled=True).astype(
        jnp.bfloat16
    )
    return (attended, block_out)


def solution(mesh):
    return jax.shard_map(
        on_device,
        mesh=mesh,
        in_specs=(
            P(("groups", "dev"), None),
            P(),
            P(None, "role", None, None),
            P("groups"),
            P("groups"),
            P("groups"),
            P(("groups", "dev"), "role", None),
            P(("groups", "dev"), "role", None, None),
            P(("groups", "dev"), None, "role", None, None),
            P(("groups", "dev")),
            P("role", None, "dev"),
        ),
        out_specs=(P(("groups", "dev"), "role", None), P(("groups", "role"), "dev")),
        check_vma=False,
    )
```

profile of v0, /device:TPU:0, one launch (start us, length us, event | category | flops | bytes accessed | tf_op | source)
XLA Modules:
  0.0 298.8 jit_solution(10407446676272909244)
XLA Ops:
  7.8 0.7 broadcast_add_fusion
  8.6 1.9 bitcast_subtract_fusion.3
  11.8 0.7 broadcast_compare_fusion
  12.5 0.9 select_reduce_fusion.2
  13.4 1.3 fusion.107
  14.8 0.6 fusion.110
  16.3 0.7 fusion.109
  17.0 0.6 fusion.108
  17.6 0.7 add.228
  18.4 0.7 gather_fusion
  19.0 0.9 fusion.46
  19.9 79.5 %psum.7 = bf16[20,1024]{1,0:T(8,128)(2,1)S(1)} all-reduce(f32[20,1024]{1,0:T(8,128)S(1)} %fusion.46), channel_id=1, replica_groups=mesh['groups'=1,'role'=2,'dev'=16] {'dev'}, use_global_device_ids=true, to_apply=%region_9.10 | all-reduce | flops 20480 | bytes 122880 | tf_op jit(solution)/shard_map/psum | solution.py:156
  99.5 7.2 %reshape.412 = bf16[4096,512]{1,0:T(8,128)(2,1)} reshape(bf16[4096,2,2,128]{3,2,1,0:T(2,128)(2,1)} %param.17) | data formatting | bytes 8388608 | tf_op jit(solution)/shard_map/reshape | solution.py:125
  106.7 6.6 %copy.138 = bf16[512,4096]{1,0:T(8,128)(2,1)} copy(bf16[512,4096]{0,1:T(8,128)(2,1)} %bitcast.222) | data formatting | bytes 8388608 | tf_op jit(solution)/shard_map/dot_general | solution.py:123
  113.8 3.6 %fusion.7 = f32[256,2,2,128]{0,3,2,1:T(8,128)S(1)} fusion(bf16[2,2,128,4096]{3,2,1,0:T(8,128)(2,1)} %bitcast.223, bf16[256,4096]{1,0:T(8,128)(2,1)S(1)} %copy-done.1, f32[4096]{0:T(1024)S(1)} %copy-done.7, f32[256]{0:T(256)S(1)} %add_rsqrt_fusion), kind=kOutput, calls=%fused_computation.18 | convolution fusion | flops 1077936128 | bytes 6833152 | tf_op jit(solution)/shard_map/dot_general | solution.py:123
  119.9 1.2 compare_and_fusion
  122.0 0.6 compare_and_fusion.3
  124.1 0.6 compare_and_fusion.1
  125.3 0.6 copy-done.2
  126.0 10.2 %fusion.106 = (bf16[16,256,2,1,128]{4,3,2,1,0:T(2,128)(2,1)}, bf16[16,256,2,1,128]{4,3,2,1,0:T(2,128)(2,1)}) fusion(bf16[16,256,2,2,128]{4,3,2,1,0:T(2,128)(2,1)} %param.23), kind=kLoop, calls=%fused_computation.189 | loop fusion | bytes 8388608 | tf_op jit(solution)/shard_map/slice | solution.py:138
  136.3 2.9 fusion.111
  140.1 37.8 %all_gather.32 = f32[16,4,5,2,4]{2,4,3,1,0:T(4,128)S(1)} all-gather(f32[1,4,5,2,4]{2,4,3,1,0:T(4,128)S(1)} %get-tuple-element.219), channel_id=1, replica_groups=mesh['groups'=1,'role'=2,'dev'=16] {'dev'}, dimensions={0}, use_global_device_ids=true | all-gather | bytes 10880 | tf_op jit(solution)/shard_map/all_gather | solution.py:12
  177.9 38.5 %all_gather.29 = f32[16,4,5,2,4]{2,4,3,1,0:T(4,128)S(1)} all-gather(f32[1,4,5,2,4]{2,4,3,1,0:T(4,128)S(1)} %get-tuple-element.220), channel_id=1, replica_groups=mesh['groups'=1,'role'=2,'dev'=16] {'dev'}, dimensions={0}, use_global_device_ids=true | all-gather | bytes 10880 | tf_op jit(solution)/shard_map/all_gather | solution.py:12
  216.5 0.9 slice_bitcast_fusion.1
  217.4 22.4 %while.19 = (s32[]{:T(128)}, f32[4,5,2,4]{1,3,2,0:T(4,128)S(1)}, f32[4,5,2,4]{1,3,2,0:T(4,128)S(1)}, f32[4,5,2,4,128]{4,3,2,1,0:T(4,128)S(1)}, f32[16,4,5,2,4]{2...) while((s32[]{:T(128)}, f32[4,5,2,4]{1,3,2,0:T(4,128)S(1)}, ...), condition=%wide.region_15.16_spmd, body=%wide.region_14.15_spmd.sunk | while | flops 62405 | bytes 254871 | solution.py:17
  217.7 1.2 fusion.123
  219.2 1.2 fusion.123
  220.7 1.2 fusion.123
  222.2 1.2 fusion.123
  223.7 1.2 fusion.123
  225.2 1.2 fusion.123
  226.7 1.2 fusion.123
  228.2 1.2 fusion.123
  229.7 1.2 fusion.123
  231.2 1.2 fusion.123
  232.7 1.2 fusion.123
  234.2 1.2 fusion.123
  235.7 1.2 fusion.123
  237.2 1.2 fusion.123
  238.7 1.2 fusion.123
  240.0 0.6 gather_fusion.2
  240.8 0.6 gather_fusion.3
  242.1 0.6 gather_fusion.1
  242.7 2.7 fusion.24
  245.4 38.6 %all_gather.36 = bf16[256,1024]{1,0:T(8,128)(2,1)S(1)} all-gather(bf16[16,1024]{1,0:T(8,128)(2,1)S(1)} %convert_element_type.68), channel_id=1, replica_groups=mesh['groups'=1,'role'=2,'dev'=16] {'dev'}, dimensions={0}, use_global_device_ids=true | all-gather | bytes 557056 | tf_op jit(solution)/shard_map/all_gather | solution.py:203
  284.0 1.0 fusion.114
  285.1 5.3 %reduce-scatter.2.cloned.1.call-done = f32[128,256]{1,0:T(8,128)} async-done(((f32[256,256]{1,0:T(8,128)}), f32[128,256]{1,0:T(8,128)}) %reduce-scatter.2.cloned.1.call-update) | async-done | bytes 131088 | tf_op jit(solution)/shard_map/reduce_scatter | solution.py:207
  290.4 1.5 convert_element_type.69
  (132 shorter events, 10.2 us)
Async XLA Ops:
  7.2 276.9 %copy-start = (bf16[8,128,256]{2,1,0:T(8,128)(2,1)S(1)}, bf16[8,128,256]{2,1,0:T(8,128)(2,1)}, u32[]{:S(2)}) copy-start(bf16[8,128,256]{2,1,0:T(8,128)(2,1)} %param.25) | copy-start | bytes 1572868
  7.2 209.3 %all-gather.2.cloned.1.call-start = ((), (), s32[]{:S(2)}) async-start(), calls=%async_computation.1 | async-start | bytes 1392640 | tf_op jit(solution)/shard_map/all_gather | solution.py:12
  106.7 6.6 %copy-start.1 = (bf16[256,4096]{1,0:T(8,128)(2,1)S(1)}, bf16[256,4096]{1,0:T(8,128)(2,1)}, u32[]{:S(2)}) copy-start(bf16[256,4096]{1,0:T(8,128)(2,1)} %param.15) | copy-start | bytes 6291460
  106.7 7.1 %copy-start.7 = (f32[4096]{0:T(1024)S(1)}, f32[4096]{0:T(1024)}, u32[]{:S(2)}) copy-start(f32[4096]{0:T(1024)} %param.16) | copy-start | bytes 49156
  125.3 0.6 copy-start.2
  125.9 10.3 %copy-start.6 = (s32[16]{0:T(128)S(1)}, s32[16]{0:T(128)}, u32[]{:S(2)}) copy-start(s32[16]{0:T(128)} %param.24) | copy-start | bytes 196
  125.9 10.3 %copy-start.5 = (bf16[16,8,128]{2,1,0:T(8,128)(2,1)S(1)}, bf16[16,8,128]{2,1,0:T(8,128)(2,1)}, u32[]{:S(2)}) copy-start(bf16[16,8,128]{2,1,0:T(8,128)(2,1)} %param.21) | copy-start | bytes 98308
  126.0 13.4 %copy-start.3 = (bf16[16,2,2,128]{3,2,1,0:T(2,128)(2,1)S(1)}, bf16[16,2,2,128]{3,2,1,0:T(2,128)(2,1)}, u32[]{:S(2)}) copy-start(bf16[16,2,2,128]{3,2,1,0:T(2,128)(2,1)} %param.22) | copy-start | bytes 49156
  126.0 164.4 %reduce-scatter.2.cloned.1.call-start = ((), (), s32[]{:S(2)}) async-start(), calls=%async_computation.2 | async-start | bytes 393216 | tf_op jit(solution)/shard_map/reduce_scatter | solution.py:207
  245.4 46.5 %copy-start.4 = (bf16[16,2,4,128]{3,2,1,0:T(4,128)(2,1)}, bf16[16,2,4,128]{3,2,1,0:T(4,128)(2,1)S(1)}, u32[]{:S(2)}) copy-start(bf16[16,2,4,128]{3,2,1,0:T(4,128)(2,1)S(1)} %fusion.24) | copy-start | bytes 98308
Sparse Core Ops, SparseCore 0:
  126.1 53.9 all-gather.1
  285.2 5.1 reduce-scatter.1
where the time goes:
time: 300 us; the launch traced here: 299 us
  blocking collectives  194 us (65%)
  local copies, waits for them, and re-layouts  37.2 us (12%)
  other arithmetic  29.3 us (10%)
  between operations  20.1 us (7%)
  matrix products  12 us (4%)
  waiting for transfers between devices  5.37 us (2%)
    psum x1, blocking collectives, on_device(): table = lax.psum(table, 'dev').astype(jnp.bfloat16)  79.5 us
    all_gather x2, blocking collectives, merged_2(): gathered = jax.tree.map(lambda a: lax.all_gather(a, axis), part)  76.3 us
    all_gather x1, blocking collectives, on_device(): lax.all_gather(flat, 'dev', axis=0, tiled=True)  38.6 us
    add x15, other arithmetic, combine(): first[2] * left_scale[..., None] + second[2] * right_scale[..., None]  17.5 us
    slice x1, local copies, waits for them, and re-layouts, on_device(): response_cache[:, :, :, 0]  10.2 us
    reshape x1, local copies, waits for them, and re-layouts, on_device(): kv_weight.reshape(width, local_heads * 2 * head_size)  7.22 us
    dot_general x1, local copies, waits for them, and re-layouts, on_device(): jnp.dot(normed, kv_weight.reshape(width, local_heads * 2 * head_size), pr...  6.6 us
  transfers between devices with their start and end apart: 2, of which 1 were waited for; matrix products, arithmetic and copies ran while one was open for 5% of the time, Pallas kernels for 0%

commit v1 on v0

--- a/solution.py
+++ b/solution.py
@@ -6,6 +6,11 @@
 RESP = 5
 PROMPT_MIN = 512
 rope_base = 500000.0
+
+
+def exchange_gather(x, name, dim):
+    stack = jnp.stack([x] * lax.axis_size(name))
+    return jnp.concatenate(lax.all_to_all(stack, name, 0, 0), axis=dim)
 
 
 def merged_2(part, axis, combine):
@@ -200,9 +205,7 @@
     flat = attended.reshape(slots, query_heads * head_size)
     weight_flat = out_weight.reshape(query_heads * head_size, out_weight.shape[2])
     head_terms = jnp.dot(
-        lax.all_gather(flat, "dev", axis=0, tiled=True),
-        weight_flat,
-        preferred_element_type=jnp.float32,
+        exchange_gather(flat, "dev", 0), weight_flat, preferred_element_type=jnp.float32
     )
     block_out = lax.psum_scatter(head_terms, "role", scatter_dimension=0, tiled=True).astype(
         jnp.bfloat16

time: 300 us -> 276 us (0.920)
  blocking collectives: 194 us -> 169 us
    all_gather x1 -> x0, blocking collectives: 38.6 us -> none  [on_device(): lax.all_gather(flat, 'dev', axis=0, tiled=True)]
    all_to_all x0 -> x1, blocking collectives: none -> 13.4 us  [exchange_gather(): return jnp.concatenate(lax.all_to_all(stack, name, 0, 0), axis=dim)]
where the time goes in v1:
time: 276 us; the launch traced here: 275 us
  blocking collectives  169 us (61%)
  local copies, waits for them, and re-layouts  37.4 us (14%)
  other arithmetic  29.3 us (11%)
  between operations  20.1 us (7%)
  matrix products  12 us (4%)
  waiting for transfers between devices  6.32 us (2%)
    psum x1, blocking collectives, on_device(): table = lax.psum(table, 'dev').astype(jnp.bfloat16)  79.5 us
    all_gather x2, blocking collectives, merged_2(): gathered = jax.tree.map(lambda a: lax.all_gather(a, axis), part)  76.2 us
    add x15, other arithmetic, combine(): first[2] * left_scale[..., None] + second[2] * right_scale[..., None]  17.5 us
    all_to_all x1, blocking collectives, exchange_gather(): return jnp.concatenate(lax.all_to_all(stack, name, 0, 0), axis=dim)  13.4 us
    slice x1, local copies, waits for them, and re-layouts, on_device(): response_cache[:, :, :, 0]  10.3 us
    reshape x1, local copies, waits for them, and re-layouts, on_device(): kv_weight.reshape(width, local_heads * 2 * head_size)  7.22 us
    dot_general x1, local copies, waits for them, and re-layouts, on_device(): jnp.dot(normed, kv_weight.reshape(width, local_heads * 2 * head_size), pr...  6.6 us
    reduce_scatter x1, waiting for transfers between devices, on_device(): lax.psum_scatter(head_terms, 'role', scatter_dimension=0, tiled=True)  6.27 us
  transfers between devices with their start and end apart: 2, of which 1 were waited for; matrix products, arithmetic and copies ran while one was open for 5% of the time, Pallas kernels for 0%

profile of v1, /device:TPU:0, one launch (start us, length us, event | category | flops | bytes accessed | tf_op | source)
XLA Modules:
  0.0 274.7 jit_solution(7736125478416696819)
XLA Ops:
  7.8 0.7 broadcast_add_fusion
  8.6 1.9 bitcast_subtract_fusion.3
  11.8 0.7 broadcast_compare_fusion
  12.5 0.9 select_reduce_fusion.2
  13.4 1.3 fusion.107
  14.8 0.6 fusion.110
  16.3 0.7 fusion.109
  17.0 0.6 fusion.108
  17.6 0.7 add.228
  18.4 0.7 gather_fusion
  19.0 0.9 fusion.46
  19.9 79.5 %psum.7 = bf16[20,1024]{1,0:T(8,128)(2,1)S(1)} all-reduce(f32[20,1024]{1,0:T(8,128)S(1)} %fusion.46), channel_id=1, replica_groups=mesh['groups'=1,'role'=2,'dev'=16] {'dev'}, use_global_device_ids=true, to_apply=%region_9.10 | all-reduce | flops 20480 | bytes 122880 | tf_op jit(solution)/shard_map/psum | solution.py:161
  99.5 7.2 %reshape.416 = bf16[4096,512]{1,0:T(8,128)(2,1)} reshape(bf16[4096,2,2,128]{3,2,1,0:T(2,128)(2,1)} %param.17) | data formatting | bytes 8388608 | tf_op jit(solution)/shard_map/reshape | solution.py:130
  106.7 6.6 %copy.138 = bf16[512,4096]{1,0:T(8,128)(2,1)} copy(bf16[512,4096]{0,1:T(8,128)(2,1)} %bitcast.223) | data formatting | bytes 8388608 | tf_op jit(solution)/shard_map/dot_general | solution.py:128
  113.8 3.6 %fusion.7 = f32[256,2,2,128]{0,3,2,1:T(8,128)S(1)} fusion(bf16[2,2,128,4096]{3,2,1,0:T(8,128)(2,1)} %bitcast.224, bf16[256,4096]{1,0:T(8,128)(2,1)S(1)} %copy-done.1, f32[4096]{0:T(1024)S(1)} %copy-done.7, f32[256]{0:T(256)S(1)} %add_rsqrt_fusion), kind=kOutput, calls=%fused_computation.18 | convolution fusion | flops 1077936128 | bytes 6833152 | tf_op jit(solution)/shard_map/dot_general | solution.py:128
  119.9 1.2 compare_and_fusion
  122.0 0.6 compare_and_fusion.3
  124.1 0.6 compare_and_fusion.1
  125.3 0.6 copy-done.2
  126.0 10.3 %fusion.106 = (bf16[16,256,2,1,128]{4,3,2,1,0:T(2,128)(2,1)}, bf16[16,256,2,1,128]{4,3,2,1,0:T(2,128)(2,1)}) fusion(bf16[16,256,2,2,128]{4,3,2,1,0:T(2,128)(2,1)} %param.23), kind=kLoop, calls=%fused_computation.189 | loop fusion | bytes 8388608 | tf_op jit(solution)/shard_map/slice | solution.py:143
  136.5 2.9 %fusion.111 = (f32[16,2,4]{2,1,0:T(2,128)S(1)}, f32[16,2,4,256]{3,2,1,0:T(4,128)S(1)}) fusion(bf16[16,2,4,128]{3,2,1,0:T(4,128)(2,1)S(1)} %bitcast.234, bf16[16,256,2,1,128]{4,3,2,1,0:T(2,128)(2,1)} %get-tuple-element.211, pred[16,256]{1,0:T(8,128)(4,1)S(1)} %iota_compare_fusion), kind=kOutput, calls=%fused_computation.194 | convolution fusion | flops 8486784 | bytes 2265600 | tf_op jit(solution)/shard_map/sngd,slnd->sngl/dot_general | solution.py:77
  140.3 37.5 %all_gather.29 = f32[16,4,5,2,4]{2,4,3,1,0:T(4,128)S(1)} all-gather(f32[1,4,5,2,4]{2,4,3,1,0:T(4,128)S(1)} %get-tuple-element.219), channel_id=1, replica_groups=mesh['groups'=1,'role'=2,'dev'=16] {'dev'}, dimensions={0}, use_global_device_ids=true | all-gather | bytes 10880 | tf_op jit(solution)/shard_map/all_gather | solution.py:17
  177.8 38.8 %all_gather.26 = f32[16,4,5,2,4]{2,4,3,1,0:T(4,128)S(1)} all-gather(f32[1,4,5,2,4]{2,4,3,1,0:T(4,128)S(1)} %get-tuple-element.220), channel_id=1, replica_groups=mesh['groups'=1,'role'=2,'dev'=16] {'dev'}, dimensions={0}, use_global_device_ids=true | all-gather | bytes 10880 | tf_op jit(solution)/shard_map/all_gather | solution.py:17
  216.6 0.9 slice_bitcast_fusion.1
  217.5 22.4 %while.19 = (s32[]{:T(128)}, f32[4,5,2,4]{1,3,2,0:T(4,128)S(1)}, f32[4,5,2,4]{1,3,2,0:T(4,128)S(1)}, f32[4,5,2,4,128]{4,3,2,1,0:T(4,128)S(1)}, f32[16,4,5,2,4]{2...) while((s32[]{:T(128)}, f32[4,5,2,4]{1,3,2,0:T(4,128)S(1)}, ...), condition=%wide.region_15.16_spmd, body=%wide.region_14.15_spmd.sunk | while | flops 62405 | bytes 254871 | solution.py:22
  217.8 1.2 fusion.123
  219.3 1.2 fusion.123
  220.8 1.2 fusion.123
  222.3 1.2 fusion.123
  223.8 1.2 fusion.123
  225.3 1.2 fusion.123
  226.8 1.2 fusion.123
  228.3 1.2 fusion.123
  229.8 1.2 fusion.123
  231.3 1.2 fusion.123
  232.8 1.2 fusion.123
  234.3 1.2 fusion.123
  235.8 1.2 fusion.123
  237.3 1.2 fusion.123
  238.8 1.2 fusion.123
  240.1 0.6 gather_fusion.2
  240.9 0.6 gather_fusion.3
  242.2 0.6 gather_fusion.1
  242.8 2.7 fusion.24
  245.6 13.4 %all_to_all.5 = bf16[16,16,1024]{2,1,0:T(8,128)(2,1)S(1)} all-to-all(bf16[16,16,1024]{2,1,0:T(8,128)(2,1)S(1)} %stack.3), channel_id=1, replica_groups=mesh['groups'=1,'role'=2,'dev'=16] {'dev'}, dimensions={0} | all-to-all | bytes 1048576 | tf_op jit(solution)/shard_map/all_to_all | solution.py:13
  259.0 1.0 fusion.114
  260.0 6.3 %reduce-scatter.2.cloned.1.call-done = f32[128,256]{1,0:T(8,128)} async-done(((f32[256,256]{1,0:T(8,128)}), f32[128,256]{1,0:T(8,128)}) %reduce-scatter.2.cloned.1.call-update) | async-done | bytes 131088 | tf_op jit(solution)/shard_map/reduce_scatter | solution.py:210
  266.3 1.5 convert_element_type.70
  (133 shorter events, 10.2 us)
Async XLA Ops:
  7.2 251.8 %copy-start = (bf16[8,128,256]{2,1,0:T(8,128)(2,1)S(1)}, bf16[8,128,256]{2,1,0:T(8,128)(2,1)}, u32[]{:S(2)}) copy-start(bf16[8,128,256]{2,1,0:T(8,128)(2,1)} %param.25) | copy-start | bytes 1572868
  7.2 209.5 %all-gather.2.cloned.1.call-start = ((), (), s32[]{:S(2)}) async-start(), calls=%async_computation.2 | async-start | bytes 1392640 | tf_op jit(solution)/shard_map/all_gather | solution.py:17
  106.7 6.6 %copy-start.1 = (bf16[256,4096]{1,0:T(8,128)(2,1)S(1)}, bf16[256,4096]{1,0:T(8,128)(2,1)}, u32[]{:S(2)}) copy-start(bf16[256,4096]{1,0:T(8,128)(2,1)} %param.15) | copy-start | bytes 6291460
  106.7 7.1 %copy-start.7 = (f32[4096]{0:T(1024)S(1)}, f32[4096]{0:T(1024)}, u32[]{:S(2)}) copy-start(f32[4096]{0:T(1024)} %param.16) | copy-start | bytes 49156
  125.3 0.6 copy-start.2
  125.9 10.4 %copy-start.6 = (s32[16]{0:T(128)S(1)}, s32[16]{0:T(128)}, u32[]{:S(2)}) copy-start(s32[16]{0:T(128)} %param.24) | copy-start | bytes 196
  125.9 10.5 %copy-start.5 = (bf16[16,8,128]{2,1,0:T(8,128)(2,1)S(1)}, bf16[16,8,128]{2,1,0:T(8,128)(2,1)}, u32[]{:S(2)}) copy-start(bf16[16,8,128]{2,1,0:T(8,128)(2,1)} %param.21) | copy-start | bytes 98308
  126.0 13.5 %copy-start.3 = (bf16[16,2,2,128]{3,2,1,0:T(2,128)(2,1)S(1)}, bf16[16,2,2,128]{3,2,1,0:T(2,128)(2,1)}, u32[]{:S(2)}) copy-start(bf16[16,2,2,128]{3,2,1,0:T(2,128)(2,1)} %param.22) | copy-start | bytes 49156
  126.0 140.3 %reduce-scatter.2.cloned.1.call-start = ((), (), s32[]{:S(2)}) async-start(), calls=%async_computation.3 | async-start | bytes 393216 | tf_op jit(solution)/shard_map/reduce_scatter | solution.py:210
  245.5 22.3 %copy-start.4 = (bf16[16,2,4,128]{3,2,1,0:T(4,128)(2,1)}, bf16[16,2,4,128]{3,2,1,0:T(4,128)(2,1)S(1)}, u32[]{:S(2)}) copy-start(bf16[16,2,4,128]{3,2,1,0:T(4,128)(2,1)S(1)} %fusion.24) | copy-start | bytes 98308
Sparse Core Ops, SparseCore 0:
  126.1 53.9 all-gather.1
  260.2 6.1 reduce-scatter.1
